TPU v7x, 256 devices: a whole 4x4x8 slice. The times are simulated.
256 devices in a mesh: ctx: 8 (over z), exp: 32 (over x, y, core).
Axes of the slice: x: 4, y: 4, z: 8, core: 2. Of those that a mesh axis runs over, the one named last changes fastest.
Arguments:
- q_latent: bfloat16 [128, 128, 512], P('exp'), may hold values from -7 to 7
- q_rope: bfloat16 [128, 64, 128], P('exp'), may hold values from -84 to 84
- cache_latent: bfloat16 [128, 4096, 512], P('exp', 'ctx'), may hold values from -6 to 6
- cache_rope: bfloat16 [128, 64, 4096], P('exp', None, 'ctx'), may hold values from -6 to 6
- lengths: int32 [128], P('exp'), may hold values from 1024 to 4096
- w_attn_out: bfloat16 [128, 512, 7168], P('ctx', None, 'exp'), may hold values from -0.1875 to 0.1875
- hidden_in: bfloat16 [128, 7168], P(None, 'exp'), may hold values from -6 to 6
- norm_gain: bfloat16 [7168], replicated, may hold values from 0.5 to 8
- w_gate: bfloat16 [32, 7168, 1024], P('exp', None, 'ctx'), may hold values from -0.0625 to 0.0625
- w_up: bfloat16 [32, 7168, 1024], P('exp', None, 'ctx'), may hold values from -0.0625 to 0.0625
- w_down: bfloat16 [32, 1024, 7168], P('exp', 'ctx'), may hold values from -0.1875 to 0.1875
- expert_ids: int32 [128, 8], replicated, may hold values from 0 to 31, all different within a row; in each aligned block of 128 rows (0 to 127, 128 to 255, ...) at most 64 rows name the same one
- gate_weights: float32 [128, 8], replicated, may hold values from 0.1 to 1
Outputs:
- layer_out: bfloat16 [128, 7168], P('exp', 'ctx')
Inputs may be any that keep to these rules, and one draw needn't show every extreme that they name: `expert_ids`: each row names 8 different experts; over all 128 rows no expert is named more than 64 times, a bound that some block reaches.
All inputs are finite; a program needn't handle non-finite values.
Results may differ from a plain program's by a relative error of at most 0.008.
Values may be sent and summed in bfloat16 or wider, within the bound.
A program may use at most 64 MiB of HBM per device.

v0:
```python
import math
import jax
import jax.numpy as jnp
from jax import lax
from jax.sharding import PartitionSpec as P

SOFTMAX_SCALE = 192.0 ** (-0.5)
MASKED = -1e30
EPSILON = 1e-06


def cut_along(array, dim, devices):
    before, after = (array.shape[:dim], array.shape[dim + 1 :])
    return jnp.moveaxis(array.reshape(*before, devices, -1, *after), dim, 0)


def summed_on_arrival(array, axis, dim):
    devices = lax.axis_size(axis)
    blocks = lax.all_to_all(cut_along(array, dim, devices), axis, 0, 0, tiled=True)
    return jnp.sum(blocks, axis=0)


def sent_together(arrays, axis, dim, along):
    widths = [math.prod(a.shape[along:]) for a in arrays]
    both = jnp.concatenate(
        [a.reshape(*a.shape[:along], w) for a, w in zip(arrays, widths)], axis=along
    )
    filled = summed_on_arrival(both, axis, dim)
    blocks = jnp.split(filled, [sum(widths[:k]) for k in range(1, len(widths))], axis=along)
    return tuple(
        (b.reshape(*filled.shape[:along], *a.shape[along:]) for a, b in zip(arrays, blocks))
    )


def copy_for_each(array, axis):
    copies = jnp.broadcast_to(array, (lax.axis_size(axis), *array.shape))
    return lax.all_to_all(copies, axis, split_axis=0, concat_axis=0, tiled=True)


def taken_together(array, axis):
    everything = copy_for_each(array, axis)
    return jnp.sum(everything, axis=0)


def slot_tables(expert_ids, gate_weights, experts, capacity):
    row_count, top_count = expert_ids.shape
    flat_ids = expert_ids.reshape(-1)
    one_hot = (flat_ids[:, None] == jnp.arange(experts, dtype=jnp.int32)[None, :]).astype(jnp.int32)
    before = jnp.cumsum(one_hot, axis=0) - one_hot
    slot_index = jnp.sum(before * one_hot, axis=1)
    target = flat_ids * capacity + slot_index
    owner_row = jnp.arange(row_count * top_count, dtype=jnp.int32) // top_count
    slot_row = jnp.full((experts * capacity,), row_count, jnp.int32).at[target].set(owner_row)
    slot_gate = (
        jnp.zeros((experts * capacity,), jnp.float32).at[target].set(gate_weights.reshape(-1))
    )
    return (slot_row, slot_gate)


def per_device(
    q_latent,
    q_rope,
    cache_latent,
    cache_rope,
    lengths,
    w_attn_out,
    hidden_in,
    norm_gain,
    w_gate,
    w_up,
    w_down,
    expert_ids,
    gate_weights,
):
    ctx_index = lax.axis_index("ctx")
    exp_index = lax.axis_index("exp")
    ctx_count = lax.axis_size("ctx")
    exp_count = lax.axis_size("exp")
    block_len = cache_latent.shape[1]
    positions = ctx_index * block_len + jnp.arange(block_len, dtype=jnp.int32)
    visible = positions[None, :] < lengths[:, None]
    scores = jnp.einsum("rhl,rpl->rhp", q_latent, cache_latent, preferred_element_type=jnp.float32)
    scores = (
        scores + jnp.einsum("rdh,rdp->rhp", q_rope, cache_rope, preferred_element_type=jnp.float32)
    ) * SOFTMAX_SCALE
    scores = jnp.where(visible[:, None, :], scores, MASKED)
    block_max = jnp.max(scores, axis=2)
    weights = jnp.where(visible[:, None, :], jnp.exp(scores - block_max[..., None]), 0.0)
    block_total = jnp.sum(weights, axis=2)
    block_value = jnp.einsum(
        "rhp,rpl->rhl",
        weights.astype(jnp.bfloat16),
        cache_latent,
        preferred_element_type=jnp.float32,
    )
    head_count = w_attn_out.shape[0]
    joint_max = lax.pmax(block_max, "ctx")
    rescale = jnp.exp(block_max - joint_max)
    share_total, share_value = sent_together(
        (block_total * rescale, block_value * rescale[..., None]), "ctx", 1, 2
    )
    attended = (share_value / share_total[..., None]).astype(jnp.bfloat16)
    latent_width = w_attn_out.shape[1]
    flat_weight = w_attn_out.reshape(head_count * latent_width, w_attn_out.shape[2])
    row_piece = lax.all_gather(attended, "exp", axis=0, tiled=True)
    partial_out = jnp.dot(
        row_piece.reshape(row_piece.shape[0], head_count * latent_width),
        flat_weight,
        preferred_element_type=jnp.float32,
    )
    hidden_state = hidden_in.astype(jnp.float32) + taken_together(partial_out, "ctx")
    row_count = hidden_in.shape[0]
    share_width = hidden_in.shape[1]
    model_width = share_width * exp_count
    column_width = model_width // ctx_count
    top_count = expert_ids.shape[1]
    local_experts = w_gate.shape[0]
    experts = exp_count * local_experts
    capacity = min(row_count, 2 * row_count * top_count // experts)
    slot_row, slot_gate = slot_tables(expert_ids, gate_weights, experts, capacity)
    rounded = hidden_state.astype(jnp.bfloat16)
    padded = jnp.concatenate([rounded, jnp.zeros((1, share_width), jnp.bfloat16)], axis=0)
    outbound = padded[slot_row].reshape(experts, capacity, share_width)
    values = lax.all_to_all(outbound, "exp", split_axis=0, concat_axis=2, tiled=True).astype(
        jnp.float32
    )
    mean_square = jnp.mean(values * values, axis=2, keepdims=True)
    normed = (values * lax.rsqrt(mean_square + EPSILON) * norm_gain.astype(jnp.float32)).astype(
        jnp.bfloat16
    )
    gate_part = jnp.einsum("end,edf->enf", normed, w_gate, preferred_element_type=jnp.float32)
    up_part = jnp.einsum("end,edf->enf", normed, w_up, preferred_element_type=jnp.float32)
    active = (jax.nn.silu(gate_part) * up_part).astype(jnp.bfloat16)
    expert_part = jnp.einsum("enf,efd->end", active, w_down, preferred_element_type=jnp.float32)
    local_rows = lax.dynamic_slice_in_dim(
        slot_row, exp_index * local_experts * capacity, local_experts * capacity
    )
    local_gates = lax.dynamic_slice_in_dim(
        slot_gate, exp_index * local_experts * capacity, local_experts * capacity
    )
    weighted = expert_part.reshape(local_experts * capacity, model_width) * local_gates[:, None]
    owner_block = exp_index * share_width // column_width
    offset = exp_index * share_width % column_width
    column_part = summed_on_arrival(weighted, "ctx", 1)
    summed = jax.ops.segment_sum(column_part, local_rows, num_segments=row_count)
    current = lax.dynamic_slice(summed, (0, offset), (row_count, share_width))
    residual = jnp.where(ctx_index == owner_block, hidden_state, 0.0)
    summed = lax.dynamic_update_slice(summed, current + residual, (0, offset))
    layer_out = summed_on_arrival(summed, "exp", 0)
    return layer_out.astype(jnp.bfloat16)


def solution(mesh):
    in_specs = (
        P("exp", None, None),
        P("exp", None, None),
        P("exp", "ctx", None),
        P("exp", None, "ctx"),
        P("exp"),
        P("ctx", None, "exp"),
        P(None, "exp"),
        P(),
        P("exp", None, "ctx"),
        P("exp", None, "ctx"),
        P("exp", "ctx", None),
        P(),
        P(),
    )
    out_specs = P("exp", "ctx")
    return jax.shard_map(
        per_device, mesh=mesh, in_specs=in_specs, out_specs=out_specs, check_vma=False
    )
```

profile of v0, /device:TPU:1, one launch (start us, length us, event | category | flops | bytes accessed | tf_op | source)
XLA Modules:
  0.0 277.0 jit_solution(6442682698349328505)
XLA Ops:
  6.5 0.9 broadcast_compare_fusion
  7.4 0.7 copy-done
  8.1 1.9 fusion.58
  10.0 0.0 copy-done.1
  10.0 0.0 copy-done.2
  10.1 0.4 fusion.57
  10.5 17.3 %pmax.7 = f32[4,128]{1,0:T(4,128)S(1)} all-reduce(f32[4,128]{1,0:T(4,128)S(1)} %get-tuple-element.7), channel_id=1, replica_groups=mesh['ctx'=8,'exp'=32] {'ctx'}, use_global_device_ids=true, to_apply=%region_6.7 | all-reduce | flops 512 | bytes 4096 | tf_op jit(solution)/shard_map/pmax | solution.py:97
  27.8 0.3 fusion.25
  28.1 1.6 convolution_multiply_fusion
  29.7 0.1 concatenate.11
  29.8 0.3 copy.64
  30.0 1.6 maximum_bitcast_fusion
  31.7 31.7 %all_to_all.29 = f32[8,4,16,513]{3,2,1,0:T(8,128)S(1)} all-to-all(f32[8,4,16,513]{3,2,1,0:T(8,128)S(1)} %maximum_bitcast_fusion), channel_id=1, replica_groups=mesh['ctx'=8,'exp'=32] {'ctx'}, dimensions={0} | all-to-all | bytes 2101248 | tf_op jit(solution)/shard_map/all_to_all | solution.py:19
  63.3 0.7 reduce_sum.68
  64.1 0.8 slice_reduce_fusion
  64.9 1.6 fusion.37
  66.6 0.0 all-gather.2.cloned.1.call-update
  66.6 51.4 %all-gather.2.cloned.1.call-done = bf16[128,16,512]{2,1,0:T(8,128)(2,1)} async-done(((bf16[4,16,512]{2,1,0:T(8,128)(2,1)}), bf16[128,16,512]{2,1,0:T(8,128)(2,1)}) %all-gather.2.cloned.1.call-update) | async-done | bytes 2097168 | tf_op jit(solution)/shard_map/all_gather | solution.py:105
  118.0 5.2 %fusion.11 = f32[128,224]{0,1:T(8,128)S(1)} fusion(bf16[16,512,224]{1,2,0:T(8,128)(2,1)} %param.18, bf16[128,16,512]{2,1,0:T(8,128)(2,1)} %all-gather.2.cloned.1.call-done), kind=kOutput, calls=%fused_computation.21 | convolution fusion | flops 469762048 | bytes 5881856 | tf_op jit(solution)/shard_map/dot_general | solution.py:106
  123.2 0.0 copy-start.4
  123.2 0.0 copy-start.3
  123.2 1.0 broadcast_in_dim.59
  124.2 6.7 %all-to-all-start.1 = ((f32[8,128,224]{1,2,0:T(8,128)}), f32[8,128,224]{1,2,0:T(8,128)S(1)}, u32[]{:S(2)}, u32[]{:S(2)}) async-start(f32[8,128,224]{1,2,0:T(8,128)} %broadcast_in_dim.59), calls=%async_computation.1 | async-start | bytes 1835008 | tf_op jit(solution)/shard_map/all_to_all | solution.py:37
  131.0 0.1 copy.59
  131.1 0.1 eq.34
  131.2 0.1 eq.30
  131.3 0.1 copy.58
  131.4 0.1 mul.116
  131.5 0.0 copy-done.3
  131.5 0.1 copy.63
  131.6 9.0 %reduce-window.6 = s32[32,8,128]{2,1,0:T(8,128)S(1)} reduce-window(s32[32,8,128]{2,1,0:T(8,128)S(1)} %fusion.38, s32[]{:T(128)} %constant.34.clone.1), window={size=1x1x128 pad=0_0x0_0x127_0}, to_apply=%region_0.1 | reduce-window | flops 4161536 | bytes 262148 | tf_op jit(solution)/shard_map/reduce-window
  140.6 0.1 slice.10
  140.7 0.1 copy.61
  140.9 0.1 copy.62
  141.0 0.1 broadcast_add_fusion
  141.1 4.3 %scatter_custom_fusion = s32[2048]{0:T(1024)S(1)} fusion(s32[1024]{0:T(1024)S(1)} %bitcast.76, s32[1024]{0:T(1024)S(1)} %add_select_fusion, s32[]{:T(128)} %constant.31.clone.1), kind=kCustom, calls=%fused_computation.66 | custom fusion | bytes 8196 | tf_op jit(solution)/shard_map/scatter | solution.py:53
  145.5 11.9 %all-to-all-done.1 = f32[8,128,224]{1,2,0:T(8,128)S(1)} async-done(((f32[8,128,224]{1,2,0:T(8,128)}), f32[8,128,224]{1,2,0:T(8,128)S(1)}, u32[]{:S(2)}, u32[]{:S(2)}) %all-to-all-start.1) | async-done | bytes 917536 | tf_op jit(solution)/shard_map/all_to_all | solution.py:37
  157.4 0.1 copy.68
  157.5 9.0 %gather_fusion = bf16[2048,224]{1,0:T(8,128)(2,1)} fusion(bf16[129,224]{1,0:T(8,128)(2,1)S(1)} %concatenate.14, s32[2048]{0:T(1024)S(1)} %fusion.46), kind=kCustom, calls=%fused_computation | custom fusion | bytes 1843200 | tf_op jit(solution)/shard_map/gather | solution.py:123
  166.5 5.6 %all-to-all-start.2 = ((bf16[32,64,224]{2,1,0:T(8,128)(2,1)}), bf16[32,64,224]{2,1,0:T(8,128)(2,1)S(1)}, u32[]{:S(2)}, u32[]{:S(2)}) async-start(bf16[32,64,224]{2,1,0:T(8,128)(2,1)} %bitcast.71), calls=%async_computation.2 | async-start | bytes 2097152 | tf_op jit(solution)/shard_map/all_to_all | solution.py:124
  172.1 0.0 copy-done.5
  172.1 0.1 reshape.209
  172.2 0.1 copy.71
  172.3 0.1 reshape.230
  172.4 4.5 %scatter_custom_fusion.1 = f32[2048]{0:T(1024)S(1)} fusion(s32[1024]{0:T(1024)S(1)} %bitcast.77, f32[1024]{0:T(1024)S(1)} %reshape.230, f32[]{:T(128)} %constant.28.clone.1), kind=kCustom, calls=%fused_computation.63 | custom fusion | bytes 8196 | tf_op jit(solution)/shard_map/scatter | solution.py:55
  176.9 3.9 %copy.72 = bf16[7168,128]{1,0:T(8,128)(2,1)} copy(bf16[7168,128]{0,1:T(8,128)(2,1)} %bitcast.72) | data formatting | bytes 3670016 | tf_op jit(solution)/shard_map/enf,efd->end/dot_general | solution.py:134
  180.9 0.1 dynamic_slice.10
  180.9 8.1 %all-to-all-done.2 = bf16[32,64,224]{2,1,0:T(8,128)(2,1)S(1)} async-done(((bf16[32,64,224]{2,1,0:T(8,128)(2,1)}), bf16[32,64,224]{2,1,0:T(8,128)(2,1)S(1)}, u32[]{:S(2)}, u32[]{:S(2)}) %all-to-all-start.2) | async-done | bytes 917536 | tf_op jit(solution)/shard_map/all_to_all | solution.py:124
  189.0 0.3 fusion
  189.4 0.3 fusion.23
  189.7 1.6 copy.69
  191.3 2.6 convert_element_type.70
  193.9 2.0 fusion.7
  195.9 4.5 %multiply_bitcast_fusion = f32[8,64,896]{2,1,0:T(8,128)} fusion(bf16[8,896,128]{2,1,0:T(8,128)(2,1)} %bitcast.69, f32[64]{0:T(128)S(1)} %dynamic_slice.10, bf16[64,7168]{1,0:T(8,128)(2,1)S(1)} %convert_element_type.70, bf16[1,7168,128]{2,1,0:T(8,128)(2,1)} %param.22, f32[64,128]{1,0:T(8,128)S(1)} %fusion.7), kind=kOutput, calls=%fused_computation.15 | convolution fusion | flops 235388928 | bytes 6455552 | tf_op jit(solution)/shard_map/enf,efd->end/dot_general | solution.py:134
  200.4 4.3 %all-to-all-start.3 = ((f32[8,64,896]{2,1,0:T(8,128)}), f32[8,64,896]{2,1,0:T(8,128)}, u32[]{:S(2)}, u32[]{:S(2)}) async-start(f32[8,64,896]{2,1,0:T(8,128)} %multiply_bitcast_fusion), calls=%async_computation.3 | async-start | bytes 3670016 | tf_op jit(solution)/shard_map/all_to_all | solution.py:19
  204.7 0.1 dynamic_slice.9
  204.8 43.0 %all-to-all-done.3 = f32[8,64,896]{2,1,0:T(8,128)} async-done(((f32[8,64,896]{2,1,0:T(8,128)}), f32[8,64,896]{2,1,0:T(8,128)}, u32[]{:S(2)}, u32[]{:S(2)}) %all-to-all-start.3) | async-done | bytes 1835040 | tf_op jit(solution)/shard_map/all_to_all | solution.py:19
  247.8 1.6 reduce_sum.71
  249.5 1.2 scatter_custom_fusion.2
  250.7 0.1 select_add_fusion
  250.8 1.3 dynamic_update_slice.3
  252.1 0.1 reshape.207
  252.2 17.2 %all_to_all.30 = f32[32,4,896]{2,1,0:T(4,128)S(1)} all-to-all(f32[32,4,896]{2,1,0:T(4,128)S(1)} %reshape.207), channel_id=1, replica_groups=mesh['ctx'=8,'exp'=32] {'exp'}, dimensions={0} | all-to-all | bytes 917504 | tf_op jit(solution)/shard_map/all_to_all | solution.py:19
  269.4 0.7 reduce_sum.72
  (22 shorter events, 0.2 us)
Async XLA Ops:
  6.5 1.6 copy-start
  6.5 111.4 %all-gather.2.cloned.1.call-start = ((), (), s32[]{:S(2)}) async-start(), calls=%async_computation.5 | async-start | bytes 2162688 | tf_op jit(solution)/shard_map/all_gather | solution.py:105
  8.1 1.9 copy-start.1
  8.1 1.9 copy-start.2
  123.2 7.7 %copy-start.4 = (s32[128,8]{0,1:T(8,128)S(1)}, s32[128,8]{0,1:T(8,128)}, u32[]{:S(2)}) copy-start(s32[128,8]{0,1:T(8,128)} %param.24) | copy-start | bytes 12292
  123.2 8.2 %copy-start.3 = (bf16[128,224]{0,1:T(8,128)(2,1)S(1)}, bf16[128,224]{0,1:T(8,128)(2,1)}, u32[]{:S(2)}) copy-start(bf16[128,224]{0,1:T(8,128)(2,1)} %param.19) | copy-start | bytes 172036
  124.2 33.1 %all-to-all-start.1 = ((f32[8,128,224]{1,2,0:T(8,128)}), f32[8,128,224]{1,2,0:T(8,128)S(1)}, u32[]{:S(2)}, u32[]{:S(2)}) async-start(f32[8,128,224]{1,2,0:T(8,128)} %broadcast_in_dim.59), calls=%async_computation.1 | async-start | bytes 1835008 | tf_op jit(solution)/shard_map/all_to_all | solution.py:37
  166.5 5.6 %copy-start.5 = (bf16[7168]{0:T(1024)(128)(2,1)S(1)}, bf16[7168]{0:T(1024)(128)(2,1)}, u32[]{:S(2)}) copy-start(bf16[7168]{0:T(1024)(128)(2,1)} %param.20) | copy-start | bytes 43012
  166.5 5.7 %copy-start.6 = (f32[128,8]{0,1:T(8,128)S(1)}, f32[128,8]{0,1:T(8,128)}, u32[]{:S(2)}) copy-start(f32[128,8]{0,1:T(8,128)} %param.25) | copy-start | bytes 12292
  166.5 22.5 %all-to-all-start.2 = ((bf16[32,64,224]{2,1,0:T(8,128)(2,1)}), bf16[32,64,224]{2,1,0:T(8,128)(2,1)S(1)}, u32[]{:S(2)}, u32[]{:S(2)}) async-start(bf16[32,64,224]{2,1,0:T(8,128)(2,1)} %bitcast.71), calls=%async_computation.2 | async-start | bytes 2097152 | tf_op jit(solution)/shard_map/all_to_all | solution.py:124
  200.4 47.5 %all-to-all-start.3 = ((f32[8,64,896]{2,1,0:T(8,128)}), f32[8,64,896]{2,1,0:T(8,128)}, u32[]{:S(2)}, u32[]{:S(2)}) async-start(f32[8,64,896]{2,1,0:T(8,128)} %multiply_bitcast_fusion), calls=%async_computation.3 | async-start | bytes 3670016 | tf_op jit(solution)/shard_map/all_to_all | solution.py:19
Sparse Core Ops, SparseCore 0:
  66.7 51.2 all-gather.1
where the time goes:
time: 278 us; the launch traced here: 277 us
  waiting for transfers between devices  114 us (41%)
  blocking collectives  66.1 us (24%)
  local copies, waits for them, and re-layouts  31.7 us (11%)
  other arithmetic  18.8 us (7%)
  starting transfers between devices  16.6 us (6%)
  matrix products  15.6 us (6%)
  between operations  13.7 us (5%)
    all_gather x1, waiting for transfers between devices, per_device(): row_piece = lax.all_gather(attended, 'exp', axis=0, tiled=True)  51.4 us
    all_to_all x2, blocking collectives, summed_on_arrival(): lax.all_to_all(cut_along(array, dim, devices), axis, 0, 0, tiled=True)  48.9 us
    all_to_all x1, waiting for transfers between devices, summed_on_arrival(): lax.all_to_all(cut_along(array, dim, devices), axis, 0, 0, tiled=True)  43 us
    pmax x1, blocking collectives, per_device(): joint_max = lax.pmax(block_max, 'ctx')  17.3 us
    all_to_all x1, waiting for transfers between devices, copy_for_each(): return lax.all_to_all(copies, axis, split_axis=0, concat_axis=0, tiled=True)  11.9 us
    another operation x3, other arithmetic  9.15 us
    gather x1, local copies, waits for them, and re-layouts, per_device(): outbound = padded[slot_row].reshape(experts, capacity, share_width)  9 us
    all_to_all x1, waiting for transfers between devices, per_device(): lax.all_to_all(outbound, 'exp', split_axis=0, concat_axis=2, tiled=True)  8.11 us
  transfers between devices with their start and end apart: 4, of which 4 were waited for; matrix products, arithmetic and copies ran while one was open for 8% of the time, Pallas kernels for 0%

commit v1 on v0

--- a/solution.py
+++ b/solution.py
@@ -7,6 +7,23 @@
 SOFTMAX_SCALE = 192.0 ** (-0.5)
 MASKED = -1e30
 EPSILON = 1e-06
+
+
+def joined_along(tiles, dim):
+    shape = list(tiles.shape[1:])
+    shape[dim] *= tiles.shape[0]
+    return jnp.moveaxis(tiles, 0, dim).reshape(shape)
+
+
+def collected_by_bits(shard, axis):
+    count, mine = (lax.axis_size(axis), lax.axis_index(axis))
+    blocks, apart = (shard[None], 1)
+    while apart < count:
+        other = lax.ppermute(blocks, axis, [(i, i ^ apart) for i in range(count)])
+        low = mine & apart == 0
+        blocks = jnp.concatenate([jnp.where(low, blocks, other), jnp.where(low, other, blocks)])
+        apart *= 2
+    return blocks
 
 
 def cut_along(array, dim, devices):
@@ -102,7 +119,7 @@
     attended = (share_value / share_total[..., None]).astype(jnp.bfloat16)
     latent_width = w_attn_out.shape[1]
     flat_weight = w_attn_out.reshape(head_count * latent_width, w_attn_out.shape[2])
-    row_piece = lax.all_gather(attended, "exp", axis=0, tiled=True)
+    row_piece = joined_along(collected_by_bits(attended, "exp"), 0)
     partial_out = jnp.dot(
         row_piece.reshape(row_piece.shape[0], head_count * latent_width),
         flat_weight,

time: 278 us -> 270 us (0.971)
  starting transfers between devices: 16.6 us -> 34.1 us
  waiting for transfers between devices: 114 us -> 98.1 us
  between operations: 13.7 us -> 0.39 us
  other arithmetic: 18.8 us -> 23.2 us
  local copies, waits for them, and re-layouts: 31.7 us -> 36 us
  matrix products: 15.6 us -> 11.5 us
    all_gather x1 -> x0, waiting for transfers between devices: 51.4 us -> none  [per_device(): row_piece = lax.all_gather(attended, 'exp', axis=0, tiled=True)]
    ppermute x0 -> x5, waiting for transfers between devices: none -> 38.3 us  [collected_by_bits(): other = lax.ppermute(blocks, axis, [(i, i ^ apart) for i in range(count)])]
    ppermute x0 -> x5, starting transfers between devices: none -> 15.1 us  [collected_by_bits(): other = lax.ppermute(blocks, axis, [(i, i ^ apart) for i in range(count)])]
    all_to_all x1, starting transfers between devices: 5.58 us -> 11.1 us  [per_device(): lax.all_to_all(outbound, 'exp', split_axis=0, concat_axis=2, tiled=True)]
    dot_general x1, matrix products: 5.24 us -> 1.2 us  [per_device(): jnp.dot(row_piece.reshape(row_piece.shape[0], head_count * latent_width),...]
    select_n x0 -> x5, other arithmetic: none -> 3.63 us  [collected_by_bits(): jnp.where(low, blocks, other)]
    all_to_all x1, waiting for transfers between devices: 11.9 us -> 8.42 us  [copy_for_each(): return lax.all_to_all(copies, axis, split_axis=0, concat_axis=0, tiled=True)]
    all_to_all x1, starting transfers between devices: 6.73 us -> 3.55 us  [copy_for_each(): return lax.all_to_all(copies, axis, split_axis=0, concat_axis=0, tiled=True)]
  transfers between devices with their start and end apart: 4 -> 8, of which waited for: 4 -> 8; matrix products, arithmetic and copies ran while one was open for 8% -> 9% of each run, Pallas kernels for 0% -> 0%
where the time goes in v1:
time: 270 us; the launch traced here: 269 us
  waiting for transfers between devices  98.1 us (36%)
  blocking collectives  66.2 us (25%)
  local copies, waits for them, and re-layouts  36 us (13%)
  starting transfers between devices  34.1 us (13%)
  other arithmetic  23.2 us (9%)
  matrix products  11.5 us (4%)
    all_to_all x2, blocking collectives, summed_on_arrival(): lax.all_to_all(cut_along(array, dim, devices), axis, 0, 0, tiled=True)  48.9 us
    all_to_all x1, waiting for transfers between devices, summed_on_arrival(): lax.all_to_all(cut_along(array, dim, devices), axis, 0, 0, tiled=True)  43.1 us
    ppermute x5, waiting for transfers between devices, collected_by_bits(): other = lax.ppermute(blocks, axis, [(i, i ^ apart) for i in range(count)])  38.3 us
    pmax x1, blocking collectives, per_device(): joint_max = lax.pmax(block_max, 'ctx')  17.3 us
    ppermute x5, starting transfers between devices, collected_by_bits(): other = lax.ppermute(blocks, axis, [(i, i ^ apart) for i in range(count)])  15.1 us
    all_to_all x1, starting transfers between devices, per_device(): lax.all_to_all(outbound, 'exp', split_axis=0, concat_axis=2, tiled=True)  11.1 us
    another operation x3, other arithmetic  9.14 us
    gather x1, local copies, waits for them, and re-layouts, per_device(): outbound = padded[slot_row].reshape(experts, capacity, share_width)  9 us
  transfers between devices with their start and end apart: 8, of which 8 were waited for; matrix products, arithmetic and copies ran while one was open for 9% of the time, Pallas kernels for 0%

profile of v1, /device:TPU:1, one launch (start us, length us, event | category | flops | bytes accessed | tf_op | source)
XLA Modules:
  0.0 269.3 jit_solution(867560357957013200)
XLA Ops:
  0.0 0.9 broadcast_compare_fusion
  0.9 0.7 copy-done
  1.6 1.8 fusion.54
  3.5 0.4 fusion.53
  3.9 17.3 %pmax.7 = f32[4,128]{1,0:T(4,128)S(1)} all-reduce(f32[4,128]{1,0:T(4,128)S(1)} %get-tuple-element.17), channel_id=1, replica_groups=mesh['ctx'=8,'exp'=32] {'ctx'}, use_global_device_ids=true, to_apply=%region_6.7 | all-reduce | flops 512 | bytes 4096 | tf_op jit(solution)/shard_map/pmax | solution.py:114
  21.2 0.3 fusion.20
  21.5 1.6 convolution_multiply_fusion
  23.2 0.3 copy.71
  23.5 1.6 maximum_bitcast_fusion
  25.1 31.7 %all_to_all.29 = f32[8,4,16,513]{3,2,1,0:T(8,128)S(1)} all-to-all(f32[8,4,16,513]{3,2,1,0:T(8,128)S(1)} %maximum_bitcast_fusion), channel_id=1, replica_groups=mesh['ctx'=8,'exp'=32] {'ctx'}, dimensions={0} | all-to-all | bytes 2101248 | tf_op jit(solution)/shard_map/all_to_all | solution.py:36
  56.7 0.7 reduce_sum.68
  57.5 0.8 slice_reduce_fusion
  58.3 1.0 fusion.35
  59.3 6.7 %collective-permute-start = (bf16[1,4,16,512]{3,2,1,0:T(8,128)(2,1)S(1)}, bf16[1,4,16,512]{3,2,1,0:T(8,128)(2,1)S(1)}, u32[]{:S(2)}, u32[]{:S(2)}) collective-permute-start(bf16[1,4,16,512]{3,2,1,0:T(8,128)(2,1)S(1)} %fusion.35), channel_id=1, source_target_pairs={{0,1},{1,0},{2,3},{3,2},{4,5},{5,4},{6,7},{7,6},{8,9},{9,8},{10,11... | collective-permute-start | bytes 196616 | tf_op jit(solution)/shard_map/ppermute | solution.py:22
  66.0 0.9 collective-permute-done
  66.9 1.0 broadcast_select_fusion.9
  68.0 1.4 collective-permute-start.1
  69.4 3.4 %collective-permute-done.1 = bf16[2,4,16,512]{3,2,1,0:T(8,128)(2,1)S(1)} collective-permute-done((bf16[2,4,16,512]{3,2,1,0:T(8,128)(2,1)S(1)}, bf16[2,4,16,512]{3,2,1,0:T(8,128)(2,1)S(1)}, u32[]{:S(2)}, u32[]{:S(2)}) %collective-permute-start.1) | collective-permute-done | bytes 131104 | tf_op jit(solution)/shard_map/ppermute | solution.py:22
  72.8 3.0 %collective-permute-start.2 = (bf16[4,4,16,512]{3,2,1,0:T(8,128)(2,1)S(1)}, bf16[4,4,16,512]{3,2,1,0:T(8,128)(2,1)S(1)}, u32[]{:S(2)}, u32[]{:S(2)}) collective-permute-start(bf16[4,4,16,512]{3,2,1,0:T(8,128)(2,1)S(1)} %pad_maximum_fusion.3), channel_id=1, source_target_pairs={{0,4},{1,5},{2,6},{3,7},{4,0},{5,1},{6,2},{7,3},{8,12},{9,13},{10,... | collective-permute-start | bytes 786440 | tf_op jit(solution)/shard_map/ppermute | solution.py:22
  75.8 5.2 %collective-permute-done.2 = bf16[4,4,16,512]{3,2,1,0:T(8,128)(2,1)S(1)} collective-permute-done((bf16[4,4,16,512]{3,2,1,0:T(8,128)(2,1)S(1)}, bf16[4,4,16,512]{3,2,1,0:T(8,128)(2,1)S(1)}, u32[]{:S(2)}, u32[]{:S(2)}) %collective-permute-start.2) | collective-permute-done | bytes 262176 | tf_op jit(solution)/shard_map/ppermute | solution.py:22
  81.1 0.7 copy-done.1
  81.9 1.3 collective-permute-start.3
  83.2 10.3 %collective-permute-done.3 = bf16[8,4,16,512]{3,2,1,0:T(8,128)(2,1)} collective-permute-done((bf16[8,4,16,512]{3,2,1,0:T(8,128)(2,1)S(1)}, bf16[8,4,16,512]{3,2,1,0:T(8,128)(2,1)}, u32[]{:S(2)}, u32[]{:S(2)}) %collective-permute-start.3) | collective-permute-done | bytes 524320 | tf_op jit(solution)/shard_map/ppermute | solution.py:22
  93.5 1.2 broadcast_select_fusion.3
  94.6 1.1 pad_maximum_fusion.1
  95.7 2.7 %collective-permute-start.4 = (bf16[16,4,16,512]{3,2,1,0:T(8,128)(2,1)}, bf16[16,4,16,512]{3,2,1,0:T(8,128)(2,1)}, u32[]{:S(2)}, u32[]{:S(2)}) collective-permute-start(bf16[16,4,16,512]{3,2,1,0:T(8,128)(2,1)} %pad_maximum_fusion.1), channel_id=1, source_target_pairs={{0,16},{1,17},{2,18},{3,19},{4,20},{5,21},{6,22},{7,23},{8,24},{9,... | collective-permute-start | bytes 3145736 | tf_op jit(solution)/shard_map/ppermute | solution.py:22
  98.5 2.4 copy.79
  100.9 18.4 %collective-permute-done.4 = bf16[16,4,16,512]{3,2,1,0:T(8,128)(2,1)} collective-permute-done((bf16[16,4,16,512]{3,2,1,0:T(8,128)(2,1)}, bf16[16,4,16,512]{3,2,1,0:T(8,128)(2,1)}, u32[]{:S(2)}, u32[]{:S(2)}) %collective-permute-start.4) | collective-permute-done | bytes 1048608 | tf_op jit(solution)/shard_map/ppermute | solution.py:22
  119.3 1.4 broadcast_select_fusion.1
  120.7 0.2 pad_maximum_fusion
  120.9 1.4 copy.81
  122.3 1.2 fusion.55
  123.5 1.0 broadcast_in_dim.63
  124.5 3.6 %all-to-all-start.1 = ((f32[8,128,224]{1,2,0:T(8,128)}), f32[8,128,224]{1,2,0:T(8,128)S(1)}, u32[]{:S(2)}, u32[]{:S(2)}) async-start(f32[8,128,224]{1,2,0:T(8,128)} %broadcast_in_dim.63), calls=%async_computation.1 | async-start | bytes 1835008 | tf_op jit(solution)/shard_map/all_to_all | solution.py:54
  128.1 0.1 copy.66
  128.4 0.1 copy.70
  128.5 9.0 %reduce-window.6 = s32[32,8,128]{2,1,0:T(8,128)S(1)} reduce-window(s32[32,8,128]{2,1,0:T(8,128)S(1)} %fusion.33, s32[]{:T(128)} %constant.31.clone.1), window={size=1x1x128 pad=0_0x0_0x127_0}, to_apply=%region_0.1 | reduce-window | flops 4161536 | bytes 262148 | tf_op jit(solution)/shard_map/reduce-window
  137.6 0.1 copy.68
  137.9 0.1 copy.65
  138.0 0.1 mul.116
  138.1 0.1 broadcast_add_fusion
  138.3 4.3 %scatter_custom_fusion = s32[2048]{0:T(1024)S(1)} fusion(s32[1024]{0:T(1024)S(1)} %bitcast.86, s32[1024]{0:T(1024)S(1)} %add_select_fusion, s32[]{:T(128)} %constant.28.clone.1), kind=kCustom, calls=%fused_computation.79 | custom fusion | bytes 8196 | tf_op jit(solution)/shard_map/scatter | solution.py:70
  142.6 8.4 %all-to-all-done.1 = f32[8,128,224]{1,2,0:T(8,128)S(1)} async-done(((f32[8,128,224]{1,2,0:T(8,128)}), f32[8,128,224]{1,2,0:T(8,128)S(1)}, u32[]{:S(2)}, u32[]{:S(2)}) %all-to-all-start.1) | async-done | bytes 917536 | tf_op jit(solution)/shard_map/all_to_all | solution.py:54
  151.2 9.0 %gather_fusion = bf16[2048,224]{1,0:T(8,128)(2,1)} fusion(bf16[129,224]{1,0:T(8,128)(2,1)S(1)} %concatenate.34, s32[2048]{0:T(1024)S(1)} %fusion.42), kind=kCustom, calls=%fused_computation | custom fusion | bytes 1843200 | tf_op jit(solution)/shard_map/gather | solution.py:140
  160.2 11.1 %all-to-all-start.2 = ((bf16[32,64,224]{2,1,0:T(8,128)(2,1)}), bf16[32,64,224]{2,1,0:T(8,128)(2,1)S(1)}, u32[]{:S(2)}, u32[]{:S(2)}) async-start(bf16[32,64,224]{2,1,0:T(8,128)(2,1)} %bitcast.80), calls=%async_computation.2 | async-start | bytes 2097152 | tf_op jit(solution)/shard_map/all_to_all | solution.py:141
  171.5 0.1 copy.77
  171.6 4.3 %scatter_custom_fusion.1 = f32[2048]{0:T(1024)S(1)} fusion(s32[1024]{0:T(1024)S(1)} %bitcast.87, f32[1024]{0:T(1024)S(1)} %reshape.232, f32[]{:T(128)} %constant.27.clone.1), kind=kCustom, calls=%fused_computation.76 | custom fusion | bytes 8196 | tf_op jit(solution)/shard_map/scatter | solution.py:72
  176.0 3.9 %copy.78 = bf16[7168,128]{1,0:T(8,128)(2,1)} copy(bf16[7168,128]{0,1:T(8,128)(2,1)} %bitcast.82) | data formatting | bytes 3670016 | tf_op jit(solution)/shard_map/enf,efd->end/dot_general | solution.py:151
  180.0 8.3 %all-to-all-done.2 = bf16[32,64,224]{2,1,0:T(8,128)(2,1)S(1)} async-done(((bf16[32,64,224]{2,1,0:T(8,128)(2,1)}), bf16[32,64,224]{2,1,0:T(8,128)(2,1)S(1)}, u32[]{:S(2)}, u32[]{:S(2)}) %all-to-all-start.2) | async-done | bytes 917536 | tf_op jit(solution)/shard_map/all_to_all | solution.py:141
  188.2 0.3 fusion
  188.6 0.3 fusion.18
  189.0 1.6 copy.75
  190.5 2.6 convert_element_type.70
  193.2 2.0 fusion.5
  195.1 4.4 %multiply_bitcast_fusion = f32[8,64,896]{2,1,0:T(8,128)} fusion(bf16[8,896,128]{2,1,0:T(8,128)(2,1)} %bitcast.78, f32[64]{0:T(128)S(1)} %dynamic_slice.10, bf16[64,7168]{1,0:T(8,128)(2,1)S(1)} %convert_element_type.70, bf16[1,7168,128]{2,1,0:T(8,128)(2,1)} %param.22, f32[64,128]{1,0:T(8,128)S(1)} %fusion.5), kind=kOutput, calls=%fused_computation.14 | convolution fusion | flops 235388928 | bytes 6455552 | tf_op jit(solution)/shard_map/enf,efd->end/dot_general | solution.py:151
  199.6 4.3 %all-to-all-start.3 = ((f32[8,64,896]{2,1,0:T(8,128)}), f32[8,64,896]{2,1,0:T(8,128)}, u32[]{:S(2)}, u32[]{:S(2)}) async-start(f32[8,64,896]{2,1,0:T(8,128)} %multiply_bitcast_fusion), calls=%async_computation.3 | async-start | bytes 3670016 | tf_op jit(solution)/shard_map/all_to_all | solution.py:36
  204.0 43.1 %all-to-all-done.3 = f32[8,64,896]{2,1,0:T(8,128)} async-done(((f32[8,64,896]{2,1,0:T(8,128)}), f32[8,64,896]{2,1,0:T(8,128)}, u32[]{:S(2)}, u32[]{:S(2)}) %all-to-all-start.3) | async-done | bytes 1835040 | tf_op jit(solution)/shard_map/all_to_all | solution.py:36
  247.0 1.6 reduce_sum.71
  248.6 1.2 scatter_custom_fusion.2
  249.9 0.1 select_add_fusion
  250.0 1.3 dynamic_update_slice.3
  251.3 0.1 reshape.209
  251.4 17.2 %all_to_all.30 = f32[32,4,896]{2,1,0:T(4,128)S(1)} all-to-all(f32[32,4,896]{2,1,0:T(4,128)S(1)} %reshape.209), channel_id=1, replica_groups=mesh['ctx'=8,'exp'=32] {'exp'}, dimensions={0} | all-to-all | bytes 917504 | tf_op jit(solution)/shard_map/all_to_all | solution.py:36
  268.7 0.7 reduce_sum.72
  (43 shorter events, 1.2 us)
Async XLA Ops:
  0.0 1.6 copy-start
  0.0 3.5 %copy-start.3 = (bf16[4,64,128]{2,1,0:T(8,128)(2,1)S(1)}, bf16[4,64,128]{2,1,0:T(8,128)(2,1)}, u32[]{:S(2)}) copy-start(bf16[4,64,128]{2,1,0:T(8,128)(2,1)} %param.14) | copy-start | bytes 196612
  0.0 3.5 %copy-start.2 = (bf16[4,64,512]{2,1,0:T(8,128)(2,1)S(1)}, bf16[4,64,512]{2,1,0:T(8,128)(2,1)}, u32[]{:S(2)}) copy-start(bf16[4,64,512]{2,1,0:T(8,128)(2,1)} %param.16) | copy-start | bytes 786436
  59.3 7.6 %collective-permute-start = (bf16[1,4,16,512]{3,2,1,0:T(8,128)(2,1)S(1)}, bf16[1,4,16,512]{3,2,1,0:T(8,128)(2,1)S(1)}, u32[]{:S(2)}, u32[]{:S(2)}) collective-permute-start(bf16[1,4,16,512]{3,2,1,0:T(8,128)(2,1)S(1)} %fusion.35), channel_id=1, source_target_pairs={{0,1},{1,0},{2,3},{3,2},{4,5},{5,4},{6,7},{7,6},{8,9},{9,8},{10,11... | collective-permute-start | bytes 196616 | tf_op jit(solution)/shard_map/ppermute | solution.py:22
  68.0 4.8 %collective-permute-start.1 = (bf16[2,4,16,512]{3,2,1,0:T(8,128)(2,1)S(1)}, bf16[2,4,16,512]{3,2,1,0:T(8,128)(2,1)S(1)}, u32[]{:S(2)}, u32[]{:S(2)}) collective-permute-start(bf16[2,4,16,512]{3,2,1,0:T(8,128)(2,1)S(1)} %pad_maximum_fusion.4), channel_id=1, source_target_pairs={{0,2},{1,3},{2,0},{3,1},{4,6},{5,7},{6,4},{7,5},{8,10},{9,11},{10,... | collective-permute-start | bytes 393224 | tf_op jit(solution)/shard_map/ppermute | solution.py:22
  72.8 8.2 %collective-permute-start.2 = (bf16[4,4,16,512]{3,2,1,0:T(8,128)(2,1)S(1)}, bf16[4,4,16,512]{3,2,1,0:T(8,128)(2,1)S(1)}, u32[]{:S(2)}, u32[]{:S(2)}) collective-permute-start(bf16[4,4,16,512]{3,2,1,0:T(8,128)(2,1)S(1)} %pad_maximum_fusion.3), channel_id=1, source_target_pairs={{0,4},{1,5},{2,6},{3,7},{4,0},{5,1},{6,2},{7,3},{8,12},{9,13},{10,... | collective-permute-start | bytes 786440 | tf_op jit(solution)/shard_map/ppermute | solution.py:22
  81.1 0.7 copy-start.1
  81.9 11.6 %collective-permute-start.3 = (bf16[8,4,16,512]{3,2,1,0:T(8,128)(2,1)S(1)}, bf16[8,4,16,512]{3,2,1,0:T(8,128)(2,1)}, u32[]{:S(2)}, u32[]{:S(2)}) collective-permute-start(bf16[8,4,16,512]{3,2,1,0:T(8,128)(2,1)S(1)} %pad_maximum_fusion.2), channel_id=1, source_target_pairs={{0,8},{1,9},{2,10},{3,11},{4,12},{5,13},{6,14},{7,15},{8,0},{9,1},... | collective-permute-start | bytes 1572872 | tf_op jit(solution)/shard_map/ppermute | solution.py:22
  95.7 23.6 %collective-permute-start.4 = (bf16[16,4,16,512]{3,2,1,0:T(8,128)(2,1)}, bf16[16,4,16,512]{3,2,1,0:T(8,128)(2,1)}, u32[]{:S(2)}, u32[]{:S(2)}) collective-permute-start(bf16[16,4,16,512]{3,2,1,0:T(8,128)(2,1)} %pad_maximum_fusion.1), channel_id=1, source_target_pairs={{0,16},{1,17},{2,18},{3,19},{4,20},{5,21},{6,22},{7,23},{8,24},{9,... | collective-permute-start | bytes 3145736 | tf_op jit(solution)/shard_map/ppermute | solution.py:22
  123.5 4.6 %copy-start.5 = (s32[128,8]{0,1:T(8,128)S(1)}, s32[128,8]{0,1:T(8,128)}, u32[]{:S(2)}) copy-start(s32[128,8]{0,1:T(8,128)} %param.24) | copy-start | bytes 12292
  123.5 4.9 %copy-start.4 = (bf16[128,224]{0,1:T(8,128)(2,1)S(1)}, bf16[128,224]{0,1:T(8,128)(2,1)}, u32[]{:S(2)}) copy-start(bf16[128,224]{0,1:T(8,128)(2,1)} %param.19) | copy-start | bytes 172036
  124.5 26.5 %all-to-all-start.1 = ((f32[8,128,224]{1,2,0:T(8,128)}), f32[8,128,224]{1,2,0:T(8,128)S(1)}, u32[]{:S(2)}, u32[]{:S(2)}) async-start(f32[8,128,224]{1,2,0:T(8,128)} %broadcast_in_dim.63), calls=%async_computation.1 | async-start | bytes 1835008 | tf_op jit(solution)/shard_map/all_to_all | solution.py:54
  160.2 11.1 %copy-start.6 = (bf16[7168]{0:T(1024)(128)(2,1)S(1)}, bf16[7168]{0:T(1024)(128)(2,1)}, u32[]{:S(2)}) copy-start(bf16[7168]{0:T(1024)(128)(2,1)} %param.20) | copy-start | bytes 43012
  160.2 11.2 %copy-start.7 = (f32[128,8]{0,1:T(8,128)S(1)}, f32[128,8]{0,1:T(8,128)}, u32[]{:S(2)}) copy-start(f32[128,8]{0,1:T(8,128)} %param.25) | copy-start | bytes 12292
  160.2 28.0 %all-to-all-start.2 = ((bf16[32,64,224]{2,1,0:T(8,128)(2,1)}), bf16[32,64,224]{2,1,0:T(8,128)(2,1)S(1)}, u32[]{:S(2)}, u32[]{:S(2)}) async-start(bf16[32,64,224]{2,1,0:T(8,128)(2,1)} %bitcast.80), calls=%async_computation.2 | async-start | bytes 2097152 | tf_op jit(solution)/shard_map/all_to_all | solution.py:141
  199.6 47.5 %all-to-all-start.3 = ((f32[8,64,896]{2,1,0:T(8,128)}), f32[8,64,896]{2,1,0:T(8,128)}, u32[]{:S(2)}, u32[]{:S(2)}) async-start(f32[8,64,896]{2,1,0:T(8,128)} %multiply_bitcast_fusion), calls=%async_computation.3 | async-start | bytes 3670016 | tf_op jit(solution)/shard_map/all_to_all | solution.py:36
